TPU v7x, 32 devices: a whole 2x2x4 slice. The times are simulated.
32 devices in a mesh: dp: 4 (over z), expert: 8 (over y, x, core).
Axes of the slice: x: 2, y: 2, z: 4, core: 2. Of those that a mesh axis runs over, the one named last changes fastest.
Arguments:
- tokens: bfloat16 [32, 212, 1024], P(('dp', 'expert')), may hold values from -6 to 6
- expert_ids: int32 [32, 212, 1], P(('dp', 'expert')), may hold values from 0 to 7; in each aligned block of 212 rows (0 to 211, 212 to 423, ..., all dimensions but the last counted through in order) at most 36 rows name the same one
- caption_lengths: int32 [32], P(('dp', 'expert')), may hold values from 1 to 16, as said below
- layer_norm_gain: float32 [1024], replicated, may hold values from 0.5 to 1.5
- router: float32 [1024, 8], replicated, may hold values from -0.1875 to 0.1875
- w_up: bfloat16 [8, 1024, 4096], P('expert', None, 'dp'), may hold values from -0.1875 to 0.1875
- w_down: bfloat16 [8, 4096, 1024], P('expert', 'dp'), may hold values from -0.09375 to 0.09375
- logit_scale: float32 [1], replicated, may hold values from 5 to 20
- logit_bias: float32 [1], replicated, may hold values from -4 to -1.5
Outputs:
- loss: float32 [1], replicated
- grad_tokens: bfloat16 [32, 212, 1024], P(('dp', 'expert'))
- grad_up: float32 [8, 1024, 4096], P('expert', None, 'dp')
- grad_down: float32 [8, 4096, 1024], P('expert', 'dp')
- grad_router: float32 [1024, 8], replicated
- layer_gain_gradient: float32 [1024], replicated
Inputs may be any that keep to these rules, and one draw needn't show every extreme that they name: `expert_ids`: among the rows of one device (aligned blocks of 212 rows, devices ordered by dp then expert) no expert is named more than 36 times, a bound that some block reaches. `caption_lengths`: some caption has all 16 tokens.
All inputs are finite; a program needn't handle non-finite values.
Results may differ from a plain program's by a relative error of at most 0.009.
Values may be sent and summed in bfloat16 or wider, within the bound.
A program may use at most 128 MiB of HBM per device.

v0:
```python
import jax
import jax.numpy as jnp
from jax import lax
from jax.sharding import PartitionSpec as P

D = 1024
PATCH = 196
CAPLEN = 16
SEQ = 212
eps = 1e-06
loss_scale = 1024.0


def gelu_slope(pre):
    return (
        0.5 * (1.0 + lax.erf(pre * 0.7071067811865476))
        + pre * jnp.exp(-0.5 * pre * pre) * 0.3989422804014327
    )


def deliver(buffer, experts, slots):
    width = buffer.shape[-1]
    sent = lax.all_to_all(
        buffer.reshape(experts, 1, slots, width), "expert", split_axis=0, concat_axis=1, tiled=True
    )
    shaped = sent.reshape(sent.shape[0], 1, sent.shape[1], slots, width)
    whole = lax.all_gather(shaped, "dp", axis=1, tiled=True)
    return whole.reshape(whole.shape[0], -1, width)


def give_back(partial_value, n_dp, n_expert, slots):
    local = partial_value.shape[0]
    width = partial_value.shape[-1]
    summed = lax.psum_scatter(
        partial_value.reshape(local, n_dp, n_expert * slots, width).astype(jnp.bfloat16),
        "dp",
        scatter_dimension=1,
        tiled=True,
    )
    rounded = summed.reshape(local, n_expert, slots, width)
    returned = lax.all_to_all(rounded, "expert", split_axis=1, concat_axis=0, tiled=True)
    return returned.reshape(-1, width)


def body(
    tokens,
    expert_ids,
    caption_lengths,
    layer_norm_gain,
    router,
    w_up,
    w_down,
    logit_scale,
    logit_bias,
):
    n_dp = lax.axis_size("dp")
    n_expert = lax.axis_size("expert")
    pair_dev = tokens.shape[0]
    rows = pair_dev * SEQ
    experts = router.shape[1]
    slots = rows * 4 // (3 * experts) + 1
    pairs_all = pair_dev * n_dp * n_expert
    input_rows = tokens.reshape(rows, D).astype(jnp.float32)
    input_mean = jnp.mean(input_rows, axis=1, keepdims=True)
    var_x = jnp.mean((input_rows - input_mean) ** 2, axis=1, keepdims=True)
    inverse_deviation = 1.0 / jnp.sqrt(var_x + eps)
    centered_scaled_input = (input_rows - input_mean) * inverse_deviation
    normalized_input = (centered_scaled_input * layer_norm_gain).astype(jnp.bfloat16)
    ids = expert_ids.reshape(rows)
    onehot = (ids[:, None] == jnp.arange(experts, dtype=jnp.int32)[None, :]).astype(jnp.int32)
    slot = jnp.sum((jnp.cumsum(onehot, axis=0) - 1) * onehot, axis=1)
    dest = ids * slots + slot
    onehot_f = onehot.astype(jnp.float32)
    buffer = jnp.zeros((experts * slots, D), jnp.bfloat16).at[dest].set(normalized_input)
    gathered = deliver(buffer, experts, slots)
    pre = jnp.einsum("erd,edf->erf", gathered, w_up, preferred_element_type=jnp.float32)
    act = jax.nn.gelu(pre, approximate=False).astype(jnp.bfloat16)
    partial_value = jnp.einsum("erf,efd->erd", act, w_down, preferred_element_type=jnp.float32)
    moe = give_back(partial_value, n_dp, n_expert, slots)[dest].astype(jnp.float32)
    xnf = normalized_input.astype(jnp.float32)
    router_logits = jnp.dot(xnf, router, precision=lax.Precision.HIGHEST)
    gate = jax.nn.sigmoid(jnp.sum(router_logits * onehot_f, axis=1))
    y = (input_rows + gate[:, None] * moe).reshape(pair_dev, SEQ, D)
    img = jnp.mean(y[:, :PATCH], axis=1)
    lengths = caption_lengths.astype(jnp.float32)
    mask = (jnp.arange(CAPLEN, dtype=jnp.int32)[None, :] < caption_lengths[:, None]).astype(
        jnp.float32
    )
    txt = jnp.sum(y[:, PATCH:] * mask[:, :, None], axis=1) / lengths[:, None]
    ru = jnp.sqrt(jnp.mean(img * img, axis=1, keepdims=True) + eps)
    rv = jnp.sqrt(jnp.mean(txt * txt, axis=1, keepdims=True) + eps)
    u = img / ru
    v = txt / rv
    scale = logit_scale[0]
    first = lax.axis_index(("dp", "expert")) * pair_dev
    mine = first + jnp.arange(pair_dev, dtype=jnp.int32)
    every = jnp.arange(pairs_all, dtype=jnp.int32)
    own_sign = jnp.where(mine[:, None] == every[None, :], 1.0, -1.0)
    u_all, v_all = (
        lax.all_gather(u, ("dp", "expert"), axis=0, tiled=True),
        lax.all_gather(v, ("dp", "expert"), axis=0, tiled=True),
    )
    logits = scale * jnp.dot(u, v_all.T, precision=lax.Precision.HIGHEST) / D + logit_bias[0]
    loss_term = -jnp.sum(jax.nn.log_sigmoid(own_sign * logits)) / pairs_all
    coef = -(loss_scale / pairs_all) * own_sign * jax.nn.sigmoid(-own_sign * logits)
    du = scale / D * jnp.dot(coef, v_all, precision=lax.Precision.HIGHEST)
    column_logits = scale * jnp.dot(u_all, v.T, precision=lax.Precision.HIGHEST) / D + logit_bias[0]
    column_sign = own_sign.T
    column_coef = (
        -(loss_scale / pairs_all) * column_sign * jax.nn.sigmoid(-column_sign * column_logits)
    )
    dv = scale / D * jnp.dot(column_coef.T, u_all, precision=lax.Precision.HIGHEST)
    dimg = (du - u * jnp.mean(du * u, axis=1, keepdims=True)) / ru
    dtxt = (dv - v * jnp.mean(dv * v, axis=1, keepdims=True)) / rv
    dy_img = jnp.broadcast_to(dimg[:, None, :] / PATCH, (pair_dev, PATCH, D))
    dy_txt = (dtxt / lengths[:, None])[:, None, :] * mask[:, :, None]
    dy = jnp.concatenate([dy_img, dy_txt], axis=1).reshape(rows, D)
    dmoe = (gate[:, None] * dy).astype(jnp.bfloat16)
    dgl = jnp.sum(dy * moe, axis=1) * gate * (1.0 - gate)
    router_part = jnp.dot(xnf.T, onehot_f * dgl[:, None], precision=lax.Precision.HIGHEST)
    grad_buffer = jnp.zeros((experts * slots, D), jnp.bfloat16).at[dest].set(dmoe)
    gathered_grads = deliver(grad_buffer, experts, slots)
    dact = jnp.einsum("erd,efd->erf", gathered_grads, w_down, preferred_element_type=jnp.float32)
    dpre = (dact * gelu_slope(pre)).astype(jnp.bfloat16)
    grad_down = jnp.einsum("erf,erd->efd", act, gathered_grads, preferred_element_type=jnp.float32)
    grad_up = jnp.einsum("erd,erf->edf", gathered, dpre, preferred_element_type=jnp.float32)
    back_partial = jnp.einsum("erf,edf->erd", dpre, w_up, preferred_element_type=jnp.float32)
    dxe = give_back(back_partial, n_dp, n_expert, slots)[dest].astype(jnp.float32)
    router_rows = jnp.dot(onehot_f, router.T, precision=lax.Precision.HIGHEST)
    gradient_normalized_input = dxe + dgl[:, None] * router_rows
    gain_partial_term = jnp.sum(gradient_normalized_input * centered_scaled_input, axis=0)
    scaled_output_gradient = gradient_normalized_input * layer_norm_gain
    normed_input_gradient = (
        scaled_output_gradient
        - jnp.mean(scaled_output_gradient, axis=1, keepdims=True)
        - centered_scaled_input
        * jnp.mean(scaled_output_gradient * centered_scaled_input, axis=1, keepdims=True)
    ) * inverse_deviation
    grad_tokens = (dy + normed_input_gradient).astype(jnp.bfloat16).reshape(pair_dev, SEQ, D)
    loss, grad_router, layer_gain_gradient = lax.psum(
        (loss_term, router_part, gain_partial_term), ("dp", "expert")
    )
    return (loss.reshape(1), grad_tokens, grad_up, grad_down, grad_router, layer_gain_gradient)


def solution(mesh):
    return jax.shard_map(
        body,
        mesh=mesh,
        in_specs=(
            P(("dp", "expert"), None, None),
            P(("dp", "expert"), None, None),
            P(("dp", "expert")),
            P(),
            P(),
            P("expert", None, "dp"),
            P("expert", "dp", None),
            P(),
            P(),
        ),
        out_specs=(
            P(),
            P(("dp", "expert"), None, None),
            P("expert", None, "dp"),
            P("expert", "dp", None),
            P(),
            P(),
        ),
        check_vma=False,
    )
```

profile of v0, /device:TPU:0, one launch (start us, length us, event | category | flops | bytes accessed | tf_op | source)
XLA Modules:
  0.0 468.2 jit_solution(15633228378693927035)
XLA Ops:
  7.2 1.3 convert_reduce_fusion
  8.5 1.3 fusion.57
  9.8 0.7 iota_compare_fusion
  10.5 0.6 reduce-window.6
  11.1 0.2 slice_reduce_fusion.1
  11.4 0.1 add_bitcast_fusion
  11.4 0.7 fusion.69
  12.1 0.7 compare_select_fusion
  12.8 2.3 scatter_custom_fusion
  15.2 0.1 reshape.514
  15.3 16.1 %all_to_all.16 = bf16[8,1,36,1024]{3,2,1,0:T(8,128)(2,1)S(1)} all-to-all(bf16[8,1,36,1024]{3,2,1,0:T(8,128)(2,1)S(1)} %bitcast.185), channel_id=1, replica_groups=mesh['dp'=4,'expert'=8] {'expert'}, dimensions={0} | all-to-all | bytes 1179648 | tf_op jit(solution)/shard_map/all_to_all | solution.py:23
  31.4 1.1 copy.16
  32.6 49.5 %all-gather.7.cloned.1.call-done = bf16[32,1,36,1024]{3,0,2,1:T(8,128)(2,1)} async-done(((bf16[8,1,36,1024]{3,0,2,1:T(8,128)(2,1)}), bf16[32,1,36,1024]{3,0,2,1:T(8,128)(2,1)}) %all-gather.7.cloned.1.call-update) | async-done | bytes 2359312 | tf_op jit(solution)/shard_map/all_gather | solution.py:27
  82.1 4.5 copy.17
  86.5 4.1 reshape.516
  90.7 14.6 %fusion.2 = (bf16[1152,1024]{1,0:T(8,128)(2,1)S(1)}, f32[1152,1024]{1,0:T(8,128)}) fusion(bf16[1152,1024]{1,0:T(8,128)(2,1)} %reshape.516, bf16[1,1024,1024]{2,1,0:T(8,128)(2,1)S(1)} %copy-done), kind=kOutput, calls=%fused_computation.9 | convolution fusion | flops 2492596224 | bytes 11534336 | tf_op jit(solution)/shard_map/erd,edf->erf/dot_general | solution.py:76
  105.3 1.5 copy-done.8
  106.7 3.8 convert_bitcast_fusion.1
  111.3 0.2 fusion.50
  111.5 45.7 %reduce-scatter.3.cloned.1.call-done = bf16[1,1,288,1024]{3,2,1,0:T(8,128)(2,1)} async-done(((bf16[1,4,288,1024]{3,2,1,0:T(8,128)(2,1)}), bf16[1,1,288,1024]{3,2,1,0:T(8,128)(2,1)}) %reduce-scatter.3.cloned.1.call-update) | async-done | bytes 589840 | tf_op jit(solution)/shard_map/reduce_scatter | solution.py:34
  157.2 2.0 reshape.519
  159.2 4.2 all-to-all-start.1
  164.8 0.5 fusion.27
  165.3 9.2 %all-to-all-done.1 = bf16[1,8,36,1024]{3,2,0,1:T(8,128)(2,1)} async-done(((bf16[1,8,36,1024]{3,2,0,1:T(8,128)(2,1)}), bf16[1,8,36,1024]{3,2,0,1:T(8,128)(2,1)}, u32[]{:S(2)}, u32[]{:S(2)}) %all-to-all-start.1) | async-done | bytes 589856 | tf_op jit(solution)/shard_map/all_to_all | solution.py:41
  174.6 1.2 reshape.520
  175.8 1.8 gather_fusion
  177.6 1.2 convert_add_fusion
  178.8 0.1 slice_reduce_fusion
  178.9 0.1 fusion.67
  179.0 0.6 multiply_reduce_fusion.3
  180.3 0.6 multiply_reduce_fusion.4
  181.6 38.6 %all-gather.1 = f32[32768]{0:T(1024)S(1)} all-gather(f32[1024]{0:T(1024)S(1)} %broadcast_divide_fusion), channel_id=3, replica_groups=mesh['dp'=4,'expert'=8] {'dp','expert'}, dimensions={0}, use_global_device_ids=true | all-gather | bytes 135168 | tf_op jit(solution)/shard_map/all_gather | solution.py:101
  220.2 37.2 %all-gather.2 = f32[32768]{0:T(1024)S(1)} all-gather(f32[1024]{0:T(1024)S(1)} %multiply_divide_fusion), channel_id=4, replica_groups=mesh['dp'=4,'expert'=8] {'dp','expert'}, dimensions={0}, use_global_device_ids=true | all-gather | bytes 135168 | tf_op jit(solution)/shard_map/all_gather | solution.py:100
  257.4 0.8 fusion.79
  258.2 0.2 fusion.80
  258.4 0.6 multiply_reduce_fusion.2
  259.7 0.2 fusion.37
  260.0 0.2 fusion.92
  260.2 0.6 multiply_reduce_fusion.1
  261.4 0.1 broadcast_multiply_fusion
  261.5 0.1 broadcast_in_dim.10
  261.6 2.4 scatter_custom_fusion.1
  264.0 2.0 reshape.523
  266.0 14.6 %all_to_all.17 = bf16[8,1,36,1024]{3,2,1,0:T(8,128)(2,1)S(1)} all-to-all(bf16[8,1,36,1024]{3,2,1,0:T(8,128)(2,1)} %bitcast.186), channel_id=1, replica_groups=mesh['dp'=4,'expert'=8] {'expert'}, dimensions={0} | all-to-all | bytes 1179648 | tf_op jit(solution)/shard_map/all_to_all | solution.py:23
  280.6 1.1 copy.20
  281.8 46.4 %all-gather.9.cloned.1.call-done = bf16[32,1,36,1024]{3,0,2,1:T(8,128)(2,1)} async-done(((bf16[8,1,36,1024]{3,0,2,1:T(8,128)(2,1)}), bf16[32,1,36,1024]{3,0,2,1:T(8,128)(2,1)}) %all-gather.9.cloned.1.call-update) | async-done | bytes 2359312 | tf_op jit(solution)/shard_map/all_gather | solution.py:27
  328.2 4.5 copy.21
  332.7 4.1 reshape.525
  336.8 6.8 %fusion.14 = bf16[1152,1024]{1,0:T(8,128)(2,1)S(1)} fusion(f32[1152,1024]{1,0:T(8,128)} %get-tuple-element.13, bf16[1152,1024]{1,0:T(8,128)(2,1)} %reshape.525, bf16[1,1024,1024]{2,1,0:T(8,128)(2,1)} %param.15), kind=kOutput, calls=%fused_computation.29 | convolution fusion | flops 2427715584 | bytes 11534336 | tf_op jit(solution)/shard_map/erd,efd->erf/dot_general | solution.py:123
  343.6 1.4 copy-done.9
  345.0 3.9 convert_bitcast_fusion
  349.6 1.2 fusion.42
  350.8 1.3 fusion.70
  352.2 7.7 %convolution_bitcast_fusion = f32[1,1024,1024]{2,1,0:T(8,128)} fusion(bf16[1152,1024]{1,0:T(8,128)(2,1)} %copy-done.8, bf16[1152,1024]{1,0:T(8,128)(2,1)} %reshape.525), kind=kOutput, calls=%fused_computation.32 | convolution fusion | flops 2415919104 | bytes 8912896 | tf_op jit(solution)/shard_map/erf,erd->efd/dot_general | solution.py:125
  359.9 35.7 %reduce-scatter.5.cloned.1.call-done = bf16[1,1,288,1024]{3,2,1,0:T(8,128)(2,1)} async-done(((bf16[1,4,288,1024]{3,2,1,0:T(8,128)(2,1)}), bf16[1,1,288,1024]{3,2,1,0:T(8,128)(2,1)}) %reduce-scatter.5.cloned.1.call-update) | async-done | bytes 589840 | tf_op jit(solution)/shard_map/reduce_scatter | solution.py:34
  395.6 2.0 reshape.526
  397.6 4.4 all-to-all-start.3
  402.0 7.3 %convolution_bitcast_fusion.1 = f32[1,1024,1024]{2,1,0:T(8,128)} fusion(bf16[1152,1024]{1,0:T(8,128)(2,1)} %reshape.516, bf16[1152,1024]{1,0:T(8,128)(2,1)} %copy-done.9), kind=kOutput, calls=%fused_computation.33 | convolution fusion | flops 2415919104 | bytes 8912896 | tf_op jit(solution)/shard_map/erd,erf->edf/dot_general | solution.py:126
  409.4 3.6 all-to-all-done.3
  413.0 1.2 reshape.527
  414.2 1.8 gather_fusion.1
  416.0 3.1 fusion.56
  419.1 40.1 %all-reduce.1 = (f32[1]{0:T(128)}, f32[1024,8]{0,1:T(8,128)}, f32[1024]{0:T(1024)}) all-reduce(f32[1]{0:T(128)} %bitcast.22, f32[1024,8]{0,1:T(8,128)S(1)} %fusion.70, f32[1024]{0:T(1024)S(1)} %get-tuple-element.6), channel_id=1, replica_groups=mesh['dp'=4,'expert'=8] {'dp','expert'}, use_global_device_ids=true, to_apply=%region_13.14 | all-reduce | flops 9217 | bytes 73736 | tf_op jit(solution)/shard_map/psum | solution.py:140
  459.2 2.5 fusion.63
  (42 shorter events, 0.5 us)
Async XLA Ops:
  7.2 83.5 %copy-start = (bf16[1,1024,1024]{2,1,0:T(8,128)(2,1)S(1)}, bf16[1,1024,1024]{2,1,0:T(8,128)(2,1)}, u32[]{:S(2)}) copy-start(bf16[1,1024,1024]{2,1,0:T(8,128)(2,1)} %param.14) | copy-start | bytes 6291460
  7.2 74.9 %all-gather.7.cloned.1.call-start = ((), (), s32[]{:S(2)}) async-start(), calls=%async_computation.8 | async-start | bytes 2949120 | tf_op jit(solution)/shard_map/all_gather | solution.py:27
  32.6 124.7 %reduce-scatter.3.cloned.1.call-start = ((), (), s32[]{:S(2)}) async-start(), calls=%async_computation.6 | async-start | bytes 2949120 | tf_op jit(solution)/shard_map/reduce_scatter | solution.py:34
  90.6 16.1 %copy-start.7 = (bf16[1,1024,1024]{2,1,0:T(8,128)(2,1)S(1)}, bf16[1,1024,1024]{2,1,0:T(8,128)(2,1)}, u32[]{:S(2)}) copy-start(bf16[1,1024,1024]{2,1,0:T(8,128)(2,1)} %param.15) | copy-start | bytes 6291460
  105.3 1.5 copy-start.8
  106.7 4.5 copy-start.1
  106.7 4.5 copy-start.4
  110.6 54.3 %copy-start.5 = (f32[1024,8]{0,1:T(8,128)S(1)}, f32[1024,8]{0,1:T(8,128)}, u32[]{:S(2)}) copy-start(f32[1024,8]{0,1:T(8,128)} %param.13) | copy-start | bytes 98308
  110.6 54.3 %copy-start.6 = (s32[1,212,1]{1,2,0:T(1,128)S(1)}, s32[1,212,1]{1,2,0:T(1,128)}, u32[]{:S(2)}) copy-start(s32[1,212,1]{1,2,0:T(1,128)} %param.10) | copy-start | bytes 2548
  111.5 53.8 %copy-start.3 = (bf16[212,1024]{1,0:T(8,128)(2,1)}, bf16[212,1024]{1,0:T(8,128)(2,1)S(1)}, u32[]{:S(2)}) copy-start(bf16[212,1024]{1,0:T(8,128)(2,1)S(1)} %fusion.50) | copy-start | bytes 1302532
  159.2 15.3 %all-to-all-start.1 = ((bf16[1,8,36,1024]{3,2,0,1:T(8,128)(2,1)}), bf16[1,8,36,1024]{3,2,0,1:T(8,128)(2,1)}, u32[]{:S(2)}, u32[]{:S(2)}) async-start(bf16[1,8,36,1024]{3,2,0,1:T(8,128)(2,1)} %bitcast.184), calls=%async_computation.2 | async-start | bytes 1310720 | tf_op jit(solution)/shard_map/all_to_all | solution.py:41
  163.4 164.8 %all-gather.9.cloned.1.call-start = ((), (), s32[]{:S(2)}) async-start(), calls=%async_computation.9 | async-start | bytes 2949120 | tf_op jit(solution)/shard_map/all_gather | solution.py:27
  261.6 88.0 %copy-start.2 = (f32[1,196,1024]{2,1,0:T(8,128)}, f32[1,196,1024]{2,1,0:T(8,128)S(1)}, u32[]{:S(2)}) copy-start(f32[1,196,1024]{2,1,0:T(8,128)S(1)} %broadcast_in_dim.10) | copy-start | bytes 2408452
  281.8 113.9 %reduce-scatter.5.cloned.1.call-start = ((), (), s32[]{:S(2)}) async-start(), calls=%async_computation.7 | async-start | bytes 2949120 | tf_op jit(solution)/shard_map/reduce_scatter | solution.py:34
  343.6 1.4 copy-start.9
  397.6 15.3 %all-to-all-start.3 = ((bf16[1,8,36,1024]{3,2,0,1:T(8,128)(2,1)}), bf16[1,8,36,1024]{3,2,0,1:T(8,128)(2,1)}, u32[]{:S(2)}, u32[]{:S(2)}) async-start(bf16[1,8,36,1024]{3,2,0,1:T(8,128)(2,1)} %bitcast.34), calls=%async_computation.5 | async-start | bytes 1310720 | tf_op jit(solution)/shard_map/all_to_all | solution.py:41
Sparse Core Ops, SparseCore 0:
  32.7 49.3 all-gather.6
  110.7 46.4 reduce-scatter.2
  281.9 46.2 all-gather.8
  349.1 46.4 reduce-scatter.4
where the time goes:
time: 470 us; the launch traced here: 468 us
  waiting for transfers between devices  190 us (40%)
  blocking collectives  147 us (31%)
  matrix products  50.6 us (11%)
  local copies, waits for them, and re-layouts  34.9 us (7%)
  between operations  19.4 us (4%)
  other arithmetic  18 us (4%)
  starting transfers between devices  8.79 us (2%)
    all_gather x2, waiting for transfers between devices, deliver(): whole = lax.all_gather(shaped, 'dp', axis=1, tiled=True)  95.9 us
    reduce_scatter x2, waiting for transfers between devices, give_back(): lax.psum_scatter(partial_value.reshape(local, n_dp, n_expert * slots, wid...  81.4 us
    psum x1, blocking collectives, body(): lax.psum((loss_term, router_part, gain_partial_term), ('dp', 'expert'))  40.1 us
    all_gather x1, blocking collectives, body(): lax.all_gather(v, ('dp', 'expert'), axis=0, tiled=True)  38.6 us
    all_gather x1, blocking collectives, body(): lax.all_gather(u, ('dp', 'expert'), axis=0, tiled=True)  37.2 us
    all_to_all x2, blocking collectives, deliver(): lax.all_to_all(buffer.reshape(experts, 1, slots, width), 'expert', split_...  30.7 us
    dot_general x1, matrix products, body(): jnp.einsum('erd,edf->erf', gathered, w_up, preferred_element_type=jnp.flo...  14.6 us
    all_to_all x2, waiting for transfers between devices, give_back(): lax.all_to_all(rounded, 'expert', split_axis=1, concat_axis=0, tiled=True)  12.8 us
  transfers between devices with their start and end apart: 6, of which 6 were waited for; matrix products, arithmetic and copies ran while one was open for 4% of the time, Pallas kernels for 0%

commit v1 on v0

--- a/solution.py
+++ b/solution.py
@@ -9,6 +9,15 @@
 SEQ = 212
 eps = 1e-06
 loss_scale = 1024.0
+counts_resolve = lambda field_in: jnp.concatenate(
+    lax.all_to_all(
+        jnp.stack(jnp.split(field_in, lax.axis_size("expert"), axis=0)),
+        axis_name="expert",
+        split_axis=0,
+        concat_axis=0,
+    ),
+    axis=1,
+)
 
 
 def gelu_slope(pre):
@@ -20,9 +29,7 @@
 
 def deliver(buffer, experts, slots):
     width = buffer.shape[-1]
-    sent = lax.all_to_all(
-        buffer.reshape(experts, 1, slots, width), "expert", split_axis=0, concat_axis=1, tiled=True
-    )
+    sent = counts_resolve(buffer.reshape(experts, 1, slots, width))
     shaped = sent.reshape(sent.shape[0], 1, sent.shape[1], slots, width)
     whole = lax.all_gather(shaped, "dp", axis=1, tiled=True)
     return whole.reshape(whole.shape[0], -1, width)

time: 470 us -> 474 us (level)
  local copies, waits for them, and re-layouts: 34.9 us -> 40.1 us
    unnamed x20 -> x34, local copies, waits for them, and re-layouts: 2.91 us -> 9.33 us
where the time goes in v1:
time: 474 us; the launch traced here: 473 us
  waiting for transfers between devices  190 us (40%)
  blocking collectives  146 us (31%)
  matrix products  50.6 us (11%)
  local copies, waits for them, and re-layouts  40.1 us (8%)
  between operations  19.4 us (4%)
  other arithmetic  18 us (4%)
  starting transfers between devices  8.79 us (2%)
    all_gather x2, waiting for transfers between devices, deliver(): whole = lax.all_gather(shaped, 'dp', axis=1, tiled=True)  95.9 us
    reduce_scatter x2, waiting for transfers between devices, give_back(): lax.psum_scatter(partial_value.reshape(local, n_dp, n_expert * slots, wid...  81.4 us
    psum x1, blocking collectives, body(): lax.psum((loss_term, router_part, gain_partial_term), ('dp', 'expert'))  40.1 us
    all_gather x1, blocking collectives, body(): lax.all_gather(v, ('dp', 'expert'), axis=0, tiled=True)  38.6 us
    all_gather x1, blocking collectives, body(): lax.all_gather(u, ('dp', 'expert'), axis=0, tiled=True)  37.2 us
    all_to_all x2, blocking collectives, lax.all_to_all(jnp.stack(jnp.split(field_in, lax.axis_size('expert'), axi...  30 us
    dot_general x1, matrix products, body(): jnp.einsum('erd,edf->erf', gathered, w_up, preferred_element_type=jnp.flo...  14.6 us
    all_to_all x2, waiting for transfers between devices, give_back(): lax.all_to_all(rounded, 'expert', split_axis=1, concat_axis=0, tiled=True)  12.8 us
  transfers between devices with their start and end apart: 6, of which 6 were waited for; matrix products, arithmetic and copies ran while one was open for 4% of the time, Pallas kernels for 0%

profile of v1, /device:TPU:0, one launch (start us, length us, event | category | flops | bytes accessed | tf_op | source)
XLA Modules:
  0.0 472.9 jit_solution(8388979983942288712)
XLA Ops:
  7.2 1.3 convert_reduce_fusion
  8.5 1.3 fusion.57
  9.8 0.7 iota_compare_fusion
  10.5 0.6 reduce-window.6
  11.1 0.2 slice_reduce_fusion.1
  11.4 0.7 fusion.85
  12.1 0.7 compare_select_fusion
  12.8 2.3 scatter_custom_fusion
  15.3 16.1 %all_to_all.28 = bf16[8,1,1,36,1024]{4,3,2,1,0:T(8,128)(2,1)S(1)} all-to-all(bf16[8,1,1,36,1024]{4,3,2,1,0:T(8,128)(2,1)S(1)} %fusion.75), channel_id=1, replica_groups=mesh['dp'=4,'expert'=8] {'expert'}, dimensions={0} | all-to-all | bytes 1179648 | tf_op jit(solution)/shard_map/all_to_all | solution.py:13
  31.5 1.1 copy.34
  32.7 49.5 %all-gather.7.cloned.1.call-done = bf16[32,1,1,36,1024]{4,0,3,2,1:T(8,128)(2,1)} async-done(((bf16[8,1,1,36,1024]{4,0,3,2,1:T(8,128)(2,1)}), bf16[32,1,1,36,1024]{4,0,3,2,1:T(8,128)(2,1)}) %all-gather.7.cloned.1.call-update) | async-done | bytes 2359312 | tf_op jit(solution)/shard_map/all_gather | solution.py:34
  82.1 4.5 copy.35
  86.6 4.1 reshape.528
  90.7 14.6 %fusion.2 = (bf16[1152,1024]{1,0:T(8,128)(2,1)S(1)}, f32[1152,1024]{1,0:T(8,128)}) fusion(bf16[1152,1024]{1,0:T(8,128)(2,1)} %reshape.528, bf16[1,1024,1024]{2,1,0:T(8,128)(2,1)S(1)} %copy-done), kind=kOutput, calls=%fused_computation.9 | convolution fusion | flops 2492596224 | bytes 11534336 | tf_op jit(solution)/shard_map/erd,edf->erf/dot_general | solution.py:83
  105.3 1.5 copy-done.8
  106.8 3.8 convert_bitcast_fusion.1
  111.3 0.2 fusion.50
  111.6 45.7 %reduce-scatter.3.cloned.1.call-done = bf16[1,1,288,1024]{3,2,1,0:T(8,128)(2,1)} async-done(((bf16[1,4,288,1024]{3,2,1,0:T(8,128)(2,1)}), bf16[1,1,288,1024]{3,2,1,0:T(8,128)(2,1)}) %reduce-scatter.3.cloned.1.call-update) | async-done | bytes 589840 | tf_op jit(solution)/shard_map/reduce_scatter | solution.py:41
  157.3 2.0 reshape.531
  159.3 4.2 all-to-all-start.1
  164.9 0.5 fusion.27
  165.4 9.2 %all-to-all-done.1 = bf16[1,8,36,1024]{3,2,0,1:T(8,128)(2,1)} async-done(((bf16[1,8,36,1024]{3,2,0,1:T(8,128)(2,1)}), bf16[1,8,36,1024]{3,2,0,1:T(8,128)(2,1)}, u32[]{:S(2)}, u32[]{:S(2)}) %all-to-all-start.1) | async-done | bytes 589856 | tf_op jit(solution)/shard_map/all_to_all | solution.py:48
  174.6 1.2 reshape.532
  175.8 1.8 gather_fusion
  177.7 1.2 convert_add_fusion
  179.0 0.6 multiply_reduce_fusion.3
  180.3 0.6 multiply_reduce_fusion.4
  181.6 38.6 %all-gather.1 = f32[32768]{0:T(1024)S(1)} all-gather(f32[1024]{0:T(1024)S(1)} %broadcast_divide_fusion), channel_id=3, replica_groups=mesh['dp'=4,'expert'=8] {'dp','expert'}, dimensions={0}, use_global_device_ids=true | all-gather | bytes 135168 | tf_op jit(solution)/shard_map/all_gather | solution.py:108
  220.3 37.2 %all-gather.2 = f32[32768]{0:T(1024)S(1)} all-gather(f32[1024]{0:T(1024)S(1)} %multiply_divide_fusion), channel_id=4, replica_groups=mesh['dp'=4,'expert'=8] {'dp','expert'}, dimensions={0}, use_global_device_ids=true | all-gather | bytes 135168 | tf_op jit(solution)/shard_map/all_gather | solution.py:107
  257.5 0.8 fusion.95
  258.5 0.6 multiply_reduce_fusion.2
  259.8 0.2 fusion.37
  260.0 0.2 fusion.108
  260.2 0.6 multiply_reduce_fusion.1
  261.7 2.4 scatter_custom_fusion.1
  264.1 0.9 fusion.74
  265.0 0.9 fusion.73
  265.9 0.9 fusion.72
  266.8 0.9 fusion.71
  267.7 0.9 fusion.70
  268.6 0.9 fusion.69
  269.5 0.9 fusion.68
  270.4 0.9 fusion.67
  271.3 13.9 %all_to_all.29 = bf16[8,1,1,36,1024]{4,3,2,1,0:T(8,128)(2,1)S(1)} all-to-all(bf16[8,1,1,36,1024]{4,3,2,1,0:T(8,128)(2,1)S(1)} %fusion.67), channel_id=1, replica_groups=mesh['dp'=4,'expert'=8] {'expert'}, dimensions={0} | all-to-all | bytes 1179648 | tf_op jit(solution)/shard_map/all_to_all | solution.py:13
  285.2 1.1 copy.37
  286.4 46.4 %all-gather.9.cloned.1.call-done = bf16[32,1,1,36,1024]{4,0,3,2,1:T(8,128)(2,1)} async-done(((bf16[8,1,1,36,1024]{4,0,3,2,1:T(8,128)(2,1)}), bf16[32,1,1,36,1024]{4,0,3,2,1:T(8,128)(2,1)}) %all-gather.9.cloned.1.call-update) | async-done | bytes 2359312 | tf_op jit(solution)/shard_map/all_gather | solution.py:34
  332.8 4.5 copy.38
  337.3 4.1 reshape.535
  341.4 6.9 %fusion.14 = bf16[1152,1024]{1,0:T(8,128)(2,1)S(1)} fusion(f32[1152,1024]{1,0:T(8,128)} %get-tuple-element.13, bf16[1152,1024]{1,0:T(8,128)(2,1)} %reshape.535, bf16[1,1024,1024]{2,1,0:T(8,128)(2,1)} %param.15), kind=kOutput, calls=%fused_computation.29 | convolution fusion | flops 2427715584 | bytes 11534336 | tf_op jit(solution)/shard_map/erd,efd->erf/dot_general | solution.py:130
  348.2 1.4 copy-done.9
  349.7 3.9 convert_bitcast_fusion
  354.3 1.2 fusion.42
  355.5 1.3 fusion.86
  356.8 7.7 %convolution_bitcast_fusion = f32[1,1024,1024]{2,1,0:T(8,128)} fusion(bf16[1152,1024]{1,0:T(8,128)(2,1)} %copy-done.8, bf16[1152,1024]{1,0:T(8,128)(2,1)} %reshape.535), kind=kOutput, calls=%fused_computation.32 | convolution fusion | flops 2415919104 | bytes 8912896 | tf_op jit(solution)/shard_map/erf,erd->efd/dot_general | solution.py:132
  364.5 35.7 %reduce-scatter.5.cloned.1.call-done = bf16[1,1,288,1024]{3,2,1,0:T(8,128)(2,1)} async-done(((bf16[1,4,288,1024]{3,2,1,0:T(8,128)(2,1)}), bf16[1,1,288,1024]{3,2,1,0:T(8,128)(2,1)}) %reduce-scatter.5.cloned.1.call-update) | async-done | bytes 589840 | tf_op jit(solution)/shard_map/reduce_scatter | solution.py:41
  400.2 2.0 reshape.536
  402.2 4.4 all-to-all-start.3
  406.7 7.3 %convolution_bitcast_fusion.1 = f32[1,1024,1024]{2,1,0:T(8,128)} fusion(bf16[1152,1024]{1,0:T(8,128)(2,1)} %reshape.528, bf16[1152,1024]{1,0:T(8,128)(2,1)} %copy-done.9), kind=kOutput, calls=%fused_computation.33 | convolution fusion | flops 2415919104 | bytes 8912896 | tf_op jit(solution)/shard_map/erd,erf->edf/dot_general | solution.py:133
  414.0 3.6 all-to-all-done.3
  417.6 1.2 reshape.537
  418.8 1.8 gather_fusion.1
  420.6 3.1 fusion.56
  423.7 40.1 %all-reduce.1 = (f32[1]{0:T(128)}, f32[1024,8]{0,1:T(8,128)}, f32[1024]{0:T(1024)}) all-reduce(f32[1]{0:T(128)} %bitcast.29, f32[1024,8]{0,1:T(8,128)S(1)} %fusion.86, f32[1024]{0:T(1024)S(1)} %get-tuple-element.6), channel_id=1, replica_groups=mesh['dp'=4,'expert'=8] {'dp','expert'}, use_global_device_ids=true, to_apply=%region_13.14 | all-reduce | flops 9217 | bytes 73736 | tf_op jit(solution)/shard_map/psum | solution.py:147
  463.8 2.5 fusion.63
  (56 shorter events, 1.1 us)
Async XLA Ops:
  7.2 83.6 %copy-start = (bf16[1,1024,1024]{2,1,0:T(8,128)(2,1)S(1)}, bf16[1,1024,1024]{2,1,0:T(8,128)(2,1)}, u32[]{:S(2)}) copy-start(bf16[1,1024,1024]{2,1,0:T(8,128)(2,1)} %param.14) | copy-start | bytes 6291460
  7.2 74.9 %all-gather.7.cloned.1.call-start = ((), (), s32[]{:S(2)}) async-start(), calls=%async_computation.8 | async-start | bytes 2949120 | tf_op jit(solution)/shard_map/all_gather | solution.py:34
  32.6 124.6 %reduce-scatter.3.cloned.1.call-start = ((), (), s32[]{:S(2)}) async-start(), calls=%async_computation.6 | async-start | bytes 2949120 | tf_op jit(solution)/shard_map/reduce_scatter | solution.py:41
  90.7 16.1 %copy-start.7 = (bf16[1,1024,1024]{2,1,0:T(8,128)(2,1)S(1)}, bf16[1,1024,1024]{2,1,0:T(8,128)(2,1)}, u32[]{:S(2)}) copy-start(bf16[1,1024,1024]{2,1,0:T(8,128)(2,1)} %param.15) | copy-start | bytes 6291460
  105.3 1.5 copy-start.8
  106.8 4.5 copy-start.1
  106.8 4.5 copy-start.4
  110.6 54.2 %copy-start.5 = (f32[1024,8]{0,1:T(8,128)S(1)}, f32[1024,8]{0,1:T(8,128)}, u32[]{:S(2)}) copy-start(f32[1024,8]{0,1:T(8,128)} %param.13) | copy-start | bytes 98308
  110.6 54.2 %copy-start.6 = (s32[1,212,1]{1,2,0:T(1,128)S(1)}, s32[1,212,1]{1,2,0:T(1,128)}, u32[]{:S(2)}) copy-start(s32[1,212,1]{1,2,0:T(1,128)} %param.10) | copy-start | bytes 2548
  111.6 53.8 %copy-start.3 = (bf16[212,1024]{1,0:T(8,128)(2,1)}, bf16[212,1024]{1,0:T(8,128)(2,1)S(1)}, u32[]{:S(2)}) copy-start(bf16[212,1024]{1,0:T(8,128)(2,1)S(1)} %fusion.50) | copy-start | bytes 1302532
  159.3 15.3 %all-to-all-start.1 = ((bf16[1,8,36,1024]{3,2,0,1:T(8,128)(2,1)}), bf16[1,8,36,1024]{3,2,0,1:T(8,128)(2,1)}, u32[]{:S(2)}, u32[]{:S(2)}) async-start(bf16[1,8,36,1024]{3,2,0,1:T(8,128)(2,1)} %bitcast.246), calls=%async_computation.2 | async-start | bytes 1310720 | tf_op jit(solution)/shard_map/all_to_all | solution.py:48
  163.5 169.3 %all-gather.9.cloned.1.call-start = ((), (), s32[]{:S(2)}) async-start(), calls=%async_computation.9 | async-start | bytes 2949120 | tf_op jit(solution)/shard_map/all_gather | solution.py:34
  261.7 92.6 %copy-start.2 = (f32[1,196,1024]{2,1,0:T(8,128)}, f32[1,196,1024]{2,1,0:T(8,128)S(1)}, u32[]{:S(2)}) copy-start(f32[1,196,1024]{2,1,0:T(8,128)S(1)} %broadcast_in_dim.10) | copy-start | bytes 2408452
  286.4 113.9 %reduce-scatter.5.cloned.1.call-start = ((), (), s32[]{:S(2)}) async-start(), calls=%async_computation.7 | async-start | bytes 2949120 | tf_op jit(solution)/shard_map/reduce_scatter | solution.py:41
  348.2 1.4 copy-start.9
  402.2 15.3 %all-to-all-start.3 = ((bf16[1,8,36,1024]{3,2,0,1:T(8,128)(2,1)}), bf16[1,8,36,1024]{3,2,0,1:T(8,128)(2,1)}, u32[]{:S(2)}, u32[]{:S(2)}) async-start(bf16[1,8,36,1024]{3,2,0,1:T(8,128)(2,1)} %bitcast.48), calls=%async_computation.5 | async-start | bytes 1310720 | tf_op jit(solution)/shard_map/all_to_all | solution.py:48
Sparse Core Ops, SparseCore 0:
  32.8 49.3 all-gather.6
  110.8 46.4 reduce-scatter.2
  286.5 46.2 all-gather.8
  353.7 46.4 reduce-scatter.4
